TPU v7x, 512 devices: a whole 4x8x8 slice. The times are simulated.
512 devices in a mesh: dp: 8 (over z), ctx: 4 (over y_lo, core), tp: 16 (over y_hi, x).
Axes of the slice: x: 4, y: 8 (y_hi: 4, y_lo: 2; y = y_hi * 2 + y_lo), z: 8, core: 2. Of those that a mesh axis runs over, the one named last changes fastest.
Arguments:
- layer_input: bfloat16 [8, 1024, 8192], P('dp', ('ctx', 'tp')), may hold values from -6 to 6
- value_weight: bfloat16 [8192, 4096], P(('dp', 'ctx'), 'tp'), may hold values from -0.0625 to 0.0625
- query_raw: bfloat16 [8, 1024, 4096], P('dp', 'ctx', 'tp'), may hold values from -6 to 6
- key_raw: bfloat16 [8, 1024, 4096], P('dp', 'ctx', 'tp'), may hold values from -6 to 6
- out_grad: bfloat16 [8, 1024, 4096], P('dp', 'ctx', 'tp'), may hold values from -6 to 6
- gate_logits: float32 [2, 8, 32, 1024], P(None, 'dp', 'tp', 'ctx'), may hold values from -14 to 4, as said below
- decay_params: float32 [2, 32], P(None, 'tp'), may hold values from -0.35 to 0.35
- saved_states: float32 [8, 4, 32, 128, 128], P('dp', 'ctx', 'tp'), may hold values from -4 to 4
Outputs:
- input_grad: bfloat16 [8, 1024, 8192], P('dp', ('ctx', 'tp'))
- query_grad: bfloat16 [8, 1024, 4096], P('dp', 'ctx', 'tp')
- key_grad: bfloat16 [8, 1024, 4096], P('dp', 'ctx', 'tp')
- gate_grad: float32 [2, 8, 32, 1024], P(None, 'dp', 'tp', 'ctx')
- decay_grad: float32 [2, 32], P(None, 'tp')
Inputs may be any that keep to these rules, and one draw needn't show every extreme that they name: `gate_logits`: row 0 holds decay logits, row 1 write-strength logits.
All inputs are finite; a program needn't handle non-finite values.
Results may differ from a plain program's by a relative error of at most 0.015.
Values may be sent and summed in bfloat16 or wider, within the bound.
A program may use at most 64 MiB of HBM per device.

v0:
```python
import jax
import jax.numpy as jnp
from jax import lax
from jax.sharding import PartitionSpec as P

SUBLEN = 64
epsilon = 1e-06


def passed_along(shard, axis, by):
    size = lax.axis_size(axis)
    pairs = [(i, i + by) for i in range(size) if 0 <= i + by < size]
    return lax.ppermute(shard, axis, pairs)


def from_everyone(shard, axis):
    copies = jnp.broadcast_to(shard, (lax.axis_size(axis), *shard.shape))
    return lax.all_to_all(copies, axis, split_axis=0, concat_axis=0, tiled=True)


def of_everyone(shard, axis):
    everything = from_everyone(shard, axis)
    return jnp.sum(everything, axis=0)


def inner_step(carried, pieces):
    query_unit, key_unit, values, log_decay, strengths = pieces
    sub_len = query_unit.shape[0]
    head_dim = query_unit.shape[1]
    cumulative = jnp.cumsum(log_decay)
    positions = jnp.arange(sub_len)
    lower_mask = positions[:, None] >= positions[None, :]
    strict_mask = positions[:, None] > positions[None, :]
    spread = jnp.where(lower_mask, cumulative[:, None] - cumulative[None, :], 0.0)
    decays = jnp.where(lower_mask, jnp.exp(spread), 0.0)
    key_gram = jnp.dot(key_unit, key_unit.T)
    system = jnp.eye(sub_len, dtype=jnp.float32) + jnp.where(
        strict_mask, strengths[:, None] * decays * key_gram, 0.0
    )
    right_side = jnp.concatenate(
        [(strengths * jnp.exp(cumulative))[:, None] * key_unit, strengths[:, None] * values], axis=1
    )
    solved = jax.scipy.linalg.solve_triangular(system, right_side, lower=True, unit_diagonal=True)
    new_values = solved[:, head_dim:] - jnp.dot(solved[:, :head_dim], carried)
    scores = decays * jnp.dot(query_unit, key_unit.T)
    output = jnp.dot(query_unit * jnp.exp(cumulative)[:, None], carried) + jnp.dot(
        scores, new_values
    )
    tail_decay = jnp.exp(cumulative[-1] - cumulative)
    updated = jnp.exp(cumulative[-1]) * carried + jnp.dot(
        (key_unit * tail_decay[:, None]).T, new_values
    )
    return (updated, output)


def core(query_row, key_row, values, gate_a, gate_b, params, initial):
    length = query_row.shape[0]
    head_dim = query_row.shape[1]
    query_unit = (
        query_row
        * lax.rsqrt(jnp.sum(query_row * query_row, axis=-1, keepdims=True) + epsilon)
        * head_dim ** (-0.5)
    )
    key_unit = key_row * lax.rsqrt(jnp.sum(key_row * key_row, axis=-1, keepdims=True) + epsilon)
    log_decay = -jnp.exp(params[0]) * jax.nn.softplus(gate_a + params[1])
    strengths = jax.nn.sigmoid(gate_b)
    blocks = length // SUBLEN

    def into_blocks(array):
        return array.reshape((blocks, SUBLEN) + array.shape[1:])

    final_state, outputs = lax.scan(
        inner_step,
        initial,
        (
            into_blocks(query_unit),
            into_blocks(key_unit),
            into_blocks(values),
            into_blocks(log_decay),
            into_blocks(strengths),
        ),
    )
    return (outputs.reshape(length, head_dim), final_state)


def core_heads(query_rows, key_rows, values, gate_a, gate_b, params, initial):
    mapped = jax.vmap(core, in_axes=(0, 0, 0, 0, 0, 1, 0))
    return mapped(query_rows, key_rows, values, gate_a, gate_b, params, initial)


def per_device(
    layer_input, value_weight, query_raw, key_raw, out_grad, gate_logits, decay_params, saved_states
):
    tokens_all = lax.all_gather(layer_input, "tp", axis=1, tiled=True)[0]
    length = tokens_all.shape[0]
    head_dim = saved_states.shape[-1]
    head_count = query_raw.shape[2] // head_dim
    weight_full = lax.all_gather(value_weight, ("dp", "ctx"), axis=0, tiled=True)
    value_flat = jnp.dot(tokens_all, weight_full, preferred_element_type=jnp.float32)
    value_round = value_flat.astype(jnp.bfloat16)

    def split_heads(flat_rows):
        return (
            flat_rows.reshape(length, head_count, head_dim).transpose(1, 0, 2).astype(jnp.float32)
        )

    query_heads = split_heads(query_raw[0])
    key_heads = split_heads(key_raw[0])
    value_heads = split_heads(value_round)
    decay_logit = gate_logits[0, 0]
    strength_logit = gate_logits[1, 0]
    initial_states = saved_states[0, 0]
    outputs, pullback = jax.vjp(
        core_heads,
        query_heads,
        key_heads,
        value_heads,
        decay_logit,
        strength_logit,
        decay_params,
        initial_states,
    )
    cotangent = split_heads(out_grad[0])
    zeros_state = jnp.zeros_like(initial_states)
    incoming = zeros_state
    for section_index in range(lax.axis_size("ctx") - 1):
        leaving = pullback((cotangent, incoming))[6]
        incoming = passed_along(leaving.astype(jnp.bfloat16), "ctx", -1).astype(leaving.dtype)
    gradients = pullback((cotangent, incoming))
    query_grad = (
        gradients[0]
        .transpose(1, 0, 2)
        .reshape(length, head_count * head_dim)
        .astype(jnp.bfloat16)[None]
    )
    key_grad = (
        gradients[1]
        .transpose(1, 0, 2)
        .reshape(length, head_count * head_dim)
        .astype(jnp.bfloat16)[None]
    )
    value_grad = (
        gradients[2].transpose(1, 0, 2).reshape(length, head_count * head_dim).astype(jnp.bfloat16)
    )
    gate_grad = jnp.stack([gradients[3], gradients[4]])[:, None]
    decay_grad = of_everyone(gradients[5], ("dp", "ctx"))
    summed = lax.psum_scatter(
        lax.dot_general(
            value_grad, weight_full, (((1,), (1,)), ((), ())), preferred_element_type=jnp.float32
        ).astype(jnp.bfloat16),
        "tp",
        scatter_dimension=0,
        tiled=True,
    )
    input_grad = summed[None]
    return (input_grad, query_grad, key_grad, gate_grad, decay_grad)


def solution(mesh):
    placed = (
        P("dp", ("ctx", "tp"), None),
        P(("dp", "ctx"), "tp"),
        P("dp", "ctx", "tp"),
        P("dp", "ctx", "tp"),
        P("dp", "ctx", "tp"),
        P(None, "dp", "tp", "ctx"),
        P(None, "tp"),
        P("dp", "ctx", "tp", None, None),
    )
    return jax.shard_map(
        per_device,
        mesh=mesh,
        in_specs=placed,
        out_specs=(
            P("dp", ("ctx", "tp"), None),
            P("dp", "ctx", "tp"),
            P("dp", "ctx", "tp"),
            P(None, "dp", "tp", "ctx"),
            P(None, "tp"),
        ),
        check_vma=False,
    )
```

profile of v0, /device:TPU:4, one launch (start us, length us, event | category | flops | bytes accessed | tf_op | source)
XLA Modules:
  0.0 489.7 jit_solution(7759611729738571562)
XLA Ops:
  13.5 79.9 %all-gather.3.cloned.1.call-done = bf16[1,256,8192]{2,1,0:T(8,128)(2,1)} async-done(((bf16[1,16,8192]{2,1,0:T(8,128)(2,1)}), bf16[1,256,8192]{2,1,0:T(8,128)(2,1)}) %all-gather.3.cloned.1.call-update) | async-done | bytes 4194320 | tf_op jit(solution)/shard_map/all_gather | solution.py:94
  93.4 74.9 %all-gather.5.cloned.1.call-done = bf16[8192,256]{1,0:T(8,128)(2,1)} async-done(((bf16[256,256]{1,0:T(8,128)(2,1)}), bf16[8192,256]{1,0:T(8,128)(2,1)}) %all-gather.5.cloned.1.call-update) | async-done | bytes 4194320 | tf_op jit(solution)/shard_map/all_gather | solution.py:98
  168.3 5.2 %fusion.210 = bf16[256,256]{0,1:T(8,128)(2,1)S(1)} fusion(bf16[8192,256]{1,0:T(8,128)(2,1)} %all-gather.5.cloned.1.call-done, bf16[1,256,8192]{2,1,0:T(8,128)(2,1)} %all-gather.3.cloned.1.call-done), kind=kOutput, calls=%fused_computation.286 | convolution fusion | flops 1073807360 | bytes 8519680 | tf_op jit(solution)/shard_map/dot_general | solution.py:99
  175.3 68.9 %while.135 = (s32[]{:T(128)}, f32[2,128,128]{2,1,0:T(8,128)S(1)}, f32[4,2,64,64]{3,2,1,0:T(8,128)}, bf16[4,2,128,64]{2,3,1,0:T(8,128)(2,1)S(1)}, f32[4,2,64,64]{...) while((s32[]{:T(128)}, f32[2,128,128]{2,1,0:T(8,128)S(1)}, ...), condition=%wide.region_4.5_spmd.clone.clone, body=%wide.region_2.4_spmd.clone.clone.sunk | while | flops 38195776 | bytes 3009961 | solution.py:72
  176.9 9.8 %custom-call.50 = f32[2,1,64,64]{2,3,1,0:T(8,128)S(1)} custom-call(f32[2,1,64,64]{3,2,1,0:T(8,128)S(1)} %add_bitcast_fusion.4), custom_call_target="InvertDiagBlocksLowerTriangular" | custom-call | tf_op jit(solution)/shard_map/jvp(vmap())/while/body/eval_jaxpr/jit(_solve_triangular)/triangular_solve | solution.py:43
  194.1 9.8 %custom-call.50 = f32[2,1,64,64]{2,3,1,0:T(8,128)S(1)} custom-call(f32[2,1,64,64]{3,2,1,0:T(8,128)S(1)} %add_bitcast_fusion.4), custom_call_target="InvertDiagBlocksLowerTriangular" | custom-call | tf_op jit(solution)/shard_map/jvp(vmap())/while/body/eval_jaxpr/jit(_solve_triangular)/triangular_solve | solution.py:43
  211.3 9.8 %custom-call.50 = f32[2,1,64,64]{2,3,1,0:T(8,128)S(1)} custom-call(f32[2,1,64,64]{3,2,1,0:T(8,128)S(1)} %add_bitcast_fusion.4), custom_call_target="InvertDiagBlocksLowerTriangular" | custom-call | tf_op jit(solution)/shard_map/jvp(vmap())/while/body/eval_jaxpr/jit(_solve_triangular)/triangular_solve | solution.py:43
  228.6 9.8 %custom-call.50 = f32[2,1,64,64]{2,3,1,0:T(8,128)S(1)} custom-call(f32[2,1,64,64]{3,2,1,0:T(8,128)S(1)} %add_bitcast_fusion.4), custom_call_target="InvertDiagBlocksLowerTriangular" | custom-call | tf_op jit(solution)/shard_map/jvp(vmap())/while/body/eval_jaxpr/jit(_solve_triangular)/triangular_solve | solution.py:43
  244.2 5.2 %while.137 = (s32[]{:T(128)}, f32[2,128,128]{2,1,0:T(8,128)S(1)}, f32[4,2,1,1]{1,3,2,0:T(1,128)}, bf16[4,2,64,128]{3,2,1,0:T(8,128)(2,1)S(1)}, bf16[4,2,64,128]{...) while((s32[]{:T(128)}, f32[2,128,128]{2,1,0:T(8,128)S(1)}, ...), condition=%wide.region_6.7_spmd.clone, body=%wide.region_5.6_spmd.clone.sunk | while | flops 14893060 | bytes 986779 | solution.py:72
  249.4 1.3 collective-permute-start
  250.7 1.8 collective-permute-done
  252.6 5.2 %while.133 = (s32[]{:T(128)}, f32[2,128,128]{2,1,0:T(8,128)S(1)}, f32[4,2,1,1]{1,3,2,0:T(1,128)}, bf16[4,2,64,128]{3,2,1,0:T(8,128)(2,1)S(1)}, bf16[4,2,64,128]{...) while((s32[]{:T(128)}, f32[2,128,128]{2,1,0:T(8,128)S(1)}, ...), condition=%wide.region_8.9_spmd, body=%wide.region_7.8_spmd.sunk | while | flops 14827523 | bytes 986249 | solution.py:72
  257.8 1.3 collective-permute-start.1
  259.1 3.9 collective-permute-done.1
  263.1 5.2 %while.134 = (s32[]{:T(128)}, f32[2,128,128]{2,1,0:T(8,128)S(1)}, f32[4,2,1,1]{1,3,2,0:T(1,128)}, bf16[4,2,64,128]{3,2,1,0:T(8,128)(2,1)S(1)}, bf16[4,2,64,128]{...) while((s32[]{:T(128)}, f32[2,128,128]{2,1,0:T(8,128)S(1)}, ...), condition=%wide.region_10.11_spmd, body=%wide.region_9.10_spmd.sunk | while | flops 14827523 | bytes 986249 | solution.py:72
  268.3 1.3 collective-permute-start.2
  270.2 3.6 collective-permute-done.2
  275.9 96.7 %while.136 = (s32[]{:T(128)}, f32[2,128,128]{2,1,0:T(8,128)S(1)}, f32[4,2,64,128]{3,2,0,1:T(8,128)}, f32[4,2,64,128]{3,2,0,1:T(8,128)}, bf16[4,2,64,128]{3,2,0,1...) while((s32[]{:T(128)}, f32[2,128,128]{2,1,0:T(8,128)S(1)}, ...), condition=%wide.region_22.23_spmd.clone.clone, body=%wide.region_11.22_spmd.clone.clone.sunk | while | flops 95114432 | bytes 4842541 | solution.py:72
  276.4 1.2 fusion.376
  279.4 9.8 %custom-call.51 = f32[2,1,64,64]{2,3,1,0:T(8,128)S(1)} custom-call(f32[2,1,64,64]{3,2,1,0:T(8,128)S(1)} %add_bitcast_fusion.5), custom_call_target="InvertDiagBlocksLowerTriangular" | custom-call | tf_op jit(solution)/shard_map/transpose(jvp(vmap()))/while/body/eval_jaxpr/jit(_solve_triangular)/triangular_solve | solution.py:43
  289.9 1.2 fusion.377
  300.5 1.2 fusion.376
  303.6 9.8 %custom-call.51 = f32[2,1,64,64]{2,3,1,0:T(8,128)S(1)} custom-call(f32[2,1,64,64]{3,2,1,0:T(8,128)S(1)} %add_bitcast_fusion.5), custom_call_target="InvertDiagBlocksLowerTriangular" | custom-call | tf_op jit(solution)/shard_map/transpose(jvp(vmap()))/while/body/eval_jaxpr/jit(_solve_triangular)/triangular_solve | solution.py:43
  314.1 1.2 fusion.377
  327.8 9.8 %custom-call.51 = f32[2,1,64,64]{2,3,1,0:T(8,128)S(1)} custom-call(f32[2,1,64,64]{3,2,1,0:T(8,128)S(1)} %add_bitcast_fusion.5), custom_call_target="InvertDiagBlocksLowerTriangular" | custom-call | tf_op jit(solution)/shard_map/transpose(jvp(vmap()))/while/body/eval_jaxpr/jit(_solve_triangular)/triangular_solve | solution.py:43
  338.3 1.2 fusion.377
  352.0 9.8 %custom-call.51 = f32[2,1,64,64]{2,3,1,0:T(8,128)S(1)} custom-call(f32[2,1,64,64]{3,2,1,0:T(8,128)S(1)} %add_bitcast_fusion.5), custom_call_target="InvertDiagBlocksLowerTriangular" | custom-call | tf_op jit(solution)/shard_map/transpose(jvp(vmap()))/while/body/eval_jaxpr/jit(_solve_triangular)/triangular_solve | solution.py:43
  362.5 1.2 fusion.377
  373.7 5.5 %convolution_convert_fusion = bf16[256,8192]{1,0:T(8,128)(2,1)} fusion(bf16[256,256]{0,1:T(8,128)(2,1)S(1)} %bitcast.659, bf16[8192,256]{1,0:T(8,128)(2,1)} %all-gather.5.cloned.1.call-done), kind=kOutput, calls=%fused_computation.283 | convolution fusion | flops 1075838976 | bytes 8519680 | tf_op jit(solution)/shard_map/dot_general | solution.py:148
  380.7 8.6 %all-to-all-start = ((f32[32,2,2]{2,1,0:T(2,128)}), f32[32,2,2]{2,1,0:T(2,128)S(1)}, u32[]{:S(2)}, u32[]{:S(2)}) async-start(f32[32,2,2]{2,1,0:T(2,128)} %broadcast_in_dim.279), calls=%async_computation.1 | async-start | bytes 65536 | tf_op jit(solution)/shard_map/all_to_all | solution.py:18
  392.3 5.3 %all-to-all-done = f32[32,2,2]{2,1,0:T(2,128)S(1)} async-done(((f32[32,2,2]{2,1,0:T(2,128)}), f32[32,2,2]{2,1,0:T(2,128)S(1)}, u32[]{:S(2)}, u32[]{:S(2)}) %all-to-all-start) | async-done | bytes 544 | tf_op jit(solution)/shard_map/all_to_all | solution.py:18
  398.2 85.0 %reduce-scatter.2.cloned.1.call-done = bf16[16,8192]{1,0:T(8,128)(2,1)} async-done(((bf16[256,8192]{1,0:T(8,128)(2,1)}), bf16[16,8192]{1,0:T(8,128)(2,1)}) %reduce-scatter.2.cloned.1.call-update) | async-done | bytes 262160 | tf_op jit(solution)/shard_map/reduce_scatter | solution.py:147
  (420 shorter events, 110.7 us)
Async XLA Ops:
  7.2 5.2 %copy-start.3 = (bf16[1,256,256]{2,1,0:T(8,128)(2,1)S(1)}, bf16[1,256,256]{2,1,0:T(8,128)(2,1)}, u32[]{:S(2)}) copy-start(bf16[1,256,256]{2,1,0:T(8,128)(2,1)} %param.22) | copy-start | bytes 393220
  7.2 5.6 %copy-start.19 = (f32[2,2]{1,0:T(2,128)S(1)}, f32[2,2]{1,0:T(2,128)}, u32[]{:S(2)}) copy-start(f32[2,2]{1,0:T(2,128)} %param.24) | copy-start | bytes 52
  7.2 86.2 %all-gather.3.cloned.1.call-start = ((), (), s32[]{:S(2)}) async-start(), calls=%async_computation.2 | async-start | bytes 4456448 | tf_op jit(solution)/shard_map/all_gather | solution.py:94
  7.9 160.4 %all-gather.5.cloned.1.call-start = ((), (), s32[]{:S(2)}) async-start(), calls=%async_computation.3 | async-start | bytes 4325376 | tf_op jit(solution)/shard_map/all_gather | solution.py:98
  8.7 474.5 %reduce-scatter.2.cloned.1.call-start = ((), (), s32[]{:S(2)}) async-start(), calls=%async_computation.4 | async-start | bytes 4456448 | tf_op jit(solution)/shard_map/reduce_scatter | solution.py:147
  9.6 2.5 copy-start.10
  10.9 1.8 copy-start.6
  10.9 1.7 copy-start.4
  12.1 0.6 copy-start.8
  12.8 160.7 %copy-start.15 = (f32[2]{0:T(128)}, f32[2]{0:T(128)S(1)}, u32[]{:S(2)}) copy-start(f32[2]{0:T(128)S(1)} %get-tuple-element.2979) | copy-start | bytes 28
  12.8 160.7 %copy-start.17 = (f32[2]{0:T(128)}, f32[2]{0:T(128)S(1)}, u32[]{:S(2)}) copy-start(f32[2]{0:T(128)S(1)} %get-tuple-element.2980) | copy-start | bytes 28
  13.5 161.8 %copy-start = (f32[1,1,2,128,128]{4,3,2,1,0:T(8,128)S(1)}, f32[1,1,2,128,128]{4,3,2,1,0:T(8,128)}, u32[]{:S(2)}) copy-start(f32[1,1,2,128,128]{4,3,2,1,0:T(8,128)} %param.25) | copy-start | bytes 393220
  249.4 3.1 collective-permute-start
  257.8 5.3 %collective-permute-start.1 = (bf16[2,128,128]{2,1,0:T(8,128)(2,1)S(1)}, bf16[2,128,128]{2,1,0:T(8,128)(2,1)S(1)}, u32[]{:S(2)}, u32[]{:S(2)}) collective-permute-start(bf16[2,128,128]{2,1,0:T(8,128)(2,1)S(1)} %convert_element_type.127), channel_id=1, source_target_pairs={{16,0},{32,16},{48,32},{17,1},{33,17},{49,33},{18,2},{34,18},{50,3... | collective-permute-start | bytes 196616 | tf_op jit(solution)/shard_map/ppermute | solution.py:13
  268.3 5.6 %collective-permute-start.2 = (bf16[2,128,128]{2,1,0:T(8,128)(2,1)S(1)}, bf16[2,128,128]{2,1,0:T(8,128)(2,1)S(1)}, u32[]{:S(2)}, u32[]{:S(2)}) collective-permute-start(bf16[2,128,128]{2,1,0:T(8,128)(2,1)S(1)} %convert_element_type.129), channel_id=1, source_target_pairs={{16,0},{32,16},{48,32},{17,1},{33,17},{49,33},{18,2},{34,18},{50,3... | collective-permute-start | bytes 196616 | tf_op jit(solution)/shard_map/ppermute | solution.py:13
  379.1 0.7 copy-start.12
  379.1 0.7 copy-start.16
  379.1 0.7 copy-start.18
  379.1 0.9 copy-start.20
  379.1 10.1 %copy-start.13 = (f32[4,2,64]{2,1,0:T(2,128)S(1)}, f32[4,2,64]{2,1,0:T(2,128)}, u32[]{:S(2)}) copy-start(f32[4,2,64]{2,1,0:T(2,128)} %get-tuple-element.1874) | copy-start | bytes 6148
  379.1 10.3 %copy-start.2 = (f32[4,2,64,128]{3,2,0,1:T(8,128)S(1)}, f32[4,2,64,128]{3,2,0,1:T(8,128)}, u32[]{:S(2)}) copy-start(f32[4,2,64,128]{3,2,0,1:T(8,128)} %get-tuple-element.1872) | copy-start | bytes 786436
  379.2 10.4 %copy-start.1 = (f32[4,2,64,128]{3,2,0,1:T(8,128)S(1)}, f32[4,2,64,128]{3,2,0,1:T(8,128)}, u32[]{:S(2)}) copy-start(f32[4,2,64,128]{3,2,0,1:T(8,128)} %get-tuple-element.1871) | copy-start | bytes 786436
  379.2 10.7 %copy-start.11 = (f32[1,1,2,256]{3,2,1,0:T(2,128)S(1)}, f32[1,1,2,256]{3,2,1,0:T(2,128)}, u32[]{:S(2)}) copy-start(f32[1,1,2,256]{3,2,1,0:T(2,128)} %copy-done.10) | copy-start | bytes 6148
  379.2 10.7 %copy-start.7 = (f32[2,256]{1,0:T(2,128)S(1)}, f32[2,256]{1,0:T(2,128)}, u32[]{:S(2)}) copy-start(f32[2,256]{1,0:T(2,128)} %copy-done.6) | copy-start | bytes 6148
  379.2 10.7 %copy-start.14 = (f32[2,1,2,256]{3,2,1,0:T(2,128)S(1)}, f32[2,1,2,256]{3,2,1,0:T(2,128)}, u32[]{:S(2)}) copy-start(f32[2,1,2,256]{3,2,1,0:T(2,128)} %param.23) | copy-start | bytes 12292
  379.2 10.8 %copy-start.9 = (f32[2,256]{1,0:T(2,128)S(1)}, f32[2,256]{1,0:T(2,128)}, u32[]{:S(2)}) copy-start(f32[2,256]{1,0:T(2,128)} %copy-done.8) | copy-start | bytes 6148
  379.2 10.8 %copy-start.5 = (f32[2,256]{1,0:T(2,128)S(1)}, f32[2,256]{1,0:T(2,128)}, u32[]{:S(2)}) copy-start(f32[2,256]{1,0:T(2,128)} %copy-done.4) | copy-start | bytes 6148
  380.7 16.9 %all-to-all-start = ((f32[32,2,2]{2,1,0:T(2,128)}), f32[32,2,2]{2,1,0:T(2,128)S(1)}, u32[]{:S(2)}, u32[]{:S(2)}) async-start(f32[32,2,2]{2,1,0:T(2,128)} %broadcast_in_dim.279), calls=%async_computation.1 | async-start | bytes 65536 | tf_op jit(solution)/shard_map/all_to_all | solution.py:18
Sparse Core Ops, SparseCore 0:
  11.0 82.3 all-gather.2
  95.6 72.6 all-gather.4
  379.4 103.7 reduce-scatter.1
where the time goes:
time: 492 us; the launch traced here: 490 us
  waiting for transfers between devices  256 us (52%)
  other arithmetic  102 us (21%)
  matrix products  63.2 us (13%)
  local copies, waits for them, and re-layouts  40.8 us (8%)
  between operations  14.5 us (3%)
  starting transfers between devices  12.6 us (3%)
    reduce_scatter x1, waiting for transfers between devices, per_device(): lax.psum_scatter(lax.dot_general(value_grad, weight_full, (((1,), (1,)),...  85 us
    another operation x36, other arithmetic, inner_step(): jax.scipy.linalg.solve_triangular(system, right_side, lower=True, unit_di...  83.2 us
    all_gather x1, waiting for transfers between devices, per_device(): tokens_all = lax.all_gather(layer_input, 'tp', axis=1, tiled=True)[0]  79.9 us
    all_gather x1, waiting for transfers between devices, per_device(): lax.all_gather(value_weight, ('dp', 'ctx'), axis=0, tiled=True)  74.9 us
    mul x16, local copies, waits for them, and re-layouts, inner_step(): jnp.exp(cumulative[-1]) * carried  10.1 us
    another operation x12, matrix products, inner_step(): jax.scipy.linalg.solve_triangular(system, right_side, lower=True, unit_di...  9.85 us
  transfers between devices with their start and end apart: 7, of which 7 were waited for; matrix products, arithmetic and copies ran while one was open for 2% of the time, Pallas kernels for 0%

commit v1 on v0

--- a/solution.py
+++ b/solution.py
@@ -95,7 +95,12 @@
     length = tokens_all.shape[0]
     head_dim = saved_states.shape[-1]
     head_count = query_raw.shape[2] // head_dim
-    weight_full = lax.all_gather(value_weight, ("dp", "ctx"), axis=0, tiled=True)
+    weight_full = jnp.concatenate(
+        lax.all_to_all(
+            jnp.stack([value_weight] * lax.axis_size(("dp", "ctx"))), ("dp", "ctx"), 0, 0
+        ),
+        axis=0,
+    )
     value_flat = jnp.dot(tokens_all, weight_full, preferred_element_type=jnp.float32)
     value_round = value_flat.astype(jnp.bfloat16)
 

time: 492 us -> 453 us (0.921)
  the two profiles are of different devices: /device:TPU:4 before, /device:TPU:6 now
where the time goes in v1:
time: 453 us; the launch traced here: 451 us
  waiting for transfers between devices  200 us (44%)
  other arithmetic  101 us (22%)
  matrix products  63.5 us (14%)
  local copies, waits for them, and re-layouts  43.8 us (10%)
  starting transfers between devices  26.3 us (6%)
  between operations  14.8 us (3%)
    all_gather x1, waiting for transfers between devices, per_device(): tokens_all = lax.all_gather(layer_input, 'tp', axis=1, tiled=True)[0]  102 us
    another operation x36, other arithmetic, inner_step(): jax.scipy.linalg.solve_triangular(system, right_side, lower=True, unit_di...  83.2 us
    reduce_scatter x1, waiting for transfers between devices, per_device(): lax.psum_scatter(lax.dot_general(value_grad, weight_full, (((1,), (1,)),...  83.1 us
    all_to_all x1, starting transfers between devices, per_device(): lax.all_to_all(jnp.stack([value_weight] * lax.axis_size(('dp', 'ctx'))),...  12 us
    all_to_all x1, starting transfers between devices, from_everyone(): return lax.all_to_all(copies, axis, split_axis=0, concat_axis=0, tiled=True)  10.3 us
    another operation x12, matrix products, inner_step(): jax.scipy.linalg.solve_triangular(system, right_side, lower=True, unit_di...  9.9 us
    mul x16, local copies, waits for them, and re-layouts, inner_step(): jnp.exp(cumulative[-1]) * carried  9.88 us
    ppermute x3, waiting for transfers between devices, passed_along(): return lax.ppermute(shard, axis, pairs)  9.17 us
  transfers between devices with their start and end apart: 7, of which 6 were waited for; matrix products, arithmetic and copies ran while one was open for 2% of the time, Pallas kernels for 0%

profile of v1, /device:TPU:6, one launch (start us, length us, event | category | flops | bytes accessed | tf_op | source)
XLA Modules:
  0.0 450.7 jit_solution(3547780723759245740)
XLA Ops:
  7.2 3.3 stack.4
  10.5 12.0 %all-to-all-start = ((bf16[32,256,256]{2,1,0:T(8,128)(2,1)}), bf16[32,256,256]{2,1,0:T(8,128)(2,1)}, u32[]{:S(2)}, u32[]{:S(2)}) async-start(bf16[32,256,256]{2,1,0:T(8,128)(2,1)} %stack.4), calls=%async_computation | async-start | bytes 8388608 | tf_op jit(solution)/shard_map/all_to_all | solution.py:99
  26.4 101.9 %all-gather.2.cloned.1.call-done = bf16[1,256,8192]{2,1,0:T(8,128)(2,1)} async-done(((bf16[1,16,8192]{2,1,0:T(8,128)(2,1)}), bf16[1,256,8192]{2,1,0:T(8,128)(2,1)}) %all-gather.2.cloned.1.call-update) | async-done | bytes 4194320 | tf_op jit(solution)/shard_map/all_gather | solution.py:94
  128.3 5.2 %fusion.210 = bf16[256,256]{0,1:T(8,128)(2,1)S(1)} fusion(bf16[8192,256]{1,0:T(8,128)(2,1)} %bitcast.23, bf16[1,256,8192]{2,1,0:T(8,128)(2,1)} %all-gather.2.cloned.1.call-done), kind=kOutput, calls=%fused_computation.286 | convolution fusion | flops 1073807360 | bytes 8519680 | tf_op jit(solution)/shard_map/dot_general | solution.py:104
  135.4 69.5 %while.135 = (s32[]{:T(128)}, f32[2,128,128]{2,1,0:T(8,128)S(1)}, f32[4,2,64,64]{3,2,1,0:T(8,128)}, bf16[4,2,128,64]{2,3,1,0:T(8,128)(2,1)S(1)}, f32[4,2,64,64]{...) while((s32[]{:T(128)}, f32[2,128,128]{2,1,0:T(8,128)S(1)}, ...), condition=%wide.region_4.5_spmd.clone.clone, body=%wide.region_2.4_spmd.clone.clone.sunk | while | flops 38195776 | bytes 3009961 | solution.py:72
  137.0 9.8 %custom-call.50 = f32[2,1,64,64]{2,3,1,0:T(8,128)S(1)} custom-call(f32[2,1,64,64]{3,2,1,0:T(8,128)S(1)} %add_bitcast_fusion.4), custom_call_target="InvertDiagBlocksLowerTriangular" | custom-call | tf_op jit(solution)/shard_map/jvp(vmap())/while/body/eval_jaxpr/jit(_solve_triangular)/triangular_solve | solution.py:43
  151.5 1.3 dynamic_update_slice.338
  154.3 9.8 %custom-call.50 = f32[2,1,64,64]{2,3,1,0:T(8,128)S(1)} custom-call(f32[2,1,64,64]{3,2,1,0:T(8,128)S(1)} %add_bitcast_fusion.4), custom_call_target="InvertDiagBlocksLowerTriangular" | custom-call | tf_op jit(solution)/shard_map/jvp(vmap())/while/body/eval_jaxpr/jit(_solve_triangular)/triangular_solve | solution.py:43
  168.8 1.3 dynamic_update_slice.338
  171.7 9.8 %custom-call.50 = f32[2,1,64,64]{2,3,1,0:T(8,128)S(1)} custom-call(f32[2,1,64,64]{3,2,1,0:T(8,128)S(1)} %add_bitcast_fusion.4), custom_call_target="InvertDiagBlocksLowerTriangular" | custom-call | tf_op jit(solution)/shard_map/jvp(vmap())/while/body/eval_jaxpr/jit(_solve_triangular)/triangular_solve | solution.py:43
  186.2 1.3 dynamic_update_slice.338
  189.1 9.8 %custom-call.50 = f32[2,1,64,64]{2,3,1,0:T(8,128)S(1)} custom-call(f32[2,1,64,64]{3,2,1,0:T(8,128)S(1)} %add_bitcast_fusion.4), custom_call_target="InvertDiagBlocksLowerTriangular" | custom-call | tf_op jit(solution)/shard_map/jvp(vmap())/while/body/eval_jaxpr/jit(_solve_triangular)/triangular_solve | solution.py:43
  203.6 1.3 dynamic_update_slice.338
  204.9 5.1 %while.137 = (s32[]{:T(128)}, f32[2,128,128]{2,1,0:T(8,128)S(1)}, f32[4,2,1,1]{1,3,2,0:T(1,128)}, bf16[4,2,64,128]{3,2,1,0:T(8,128)(2,1)S(1)}, bf16[4,2,64,128]{...) while((s32[]{:T(128)}, f32[2,128,128]{2,1,0:T(8,128)S(1)}, ...), condition=%wide.region_6.7_spmd.clone, body=%wide.region_5.6_spmd.clone.sunk | while | flops 14893060 | bytes 986779 | solution.py:72
  210.1 1.3 collective-permute-start
  211.4 1.8 collective-permute-done
  213.2 5.1 %while.133 = (s32[]{:T(128)}, f32[2,128,128]{2,1,0:T(8,128)S(1)}, f32[4,2,1,1]{1,3,2,0:T(1,128)}, bf16[4,2,64,128]{3,2,1,0:T(8,128)(2,1)S(1)}, bf16[4,2,64,128]{...) while((s32[]{:T(128)}, f32[2,128,128]{2,1,0:T(8,128)S(1)}, ...), condition=%wide.region_8.9_spmd, body=%wide.region_7.8_spmd.sunk | while | flops 14827523 | bytes 986249 | solution.py:72
  218.4 1.3 collective-permute-start.1
  219.7 3.7 collective-permute-done.1
  223.5 5.1 %while.134 = (s32[]{:T(128)}, f32[2,128,128]{2,1,0:T(8,128)S(1)}, f32[4,2,1,1]{1,3,2,0:T(1,128)}, bf16[4,2,64,128]{3,2,1,0:T(8,128)(2,1)S(1)}, bf16[4,2,64,128]{...) while((s32[]{:T(128)}, f32[2,128,128]{2,1,0:T(8,128)S(1)}, ...), condition=%wide.region_10.11_spmd, body=%wide.region_9.10_spmd.sunk | while | flops 14827523 | bytes 986249 | solution.py:72
  228.6 1.3 collective-permute-start.2
  230.6 3.6 collective-permute-done.2
  236.3 97.1 %while.136 = (s32[]{:T(128)}, f32[2,128,128]{2,1,0:T(8,128)S(1)}, f32[4,2,64,128]{3,2,0,1:T(8,128)}, f32[4,2,64,128]{3,2,0,1:T(8,128)}, bf16[4,2,64,128]{3,2,0,1...) while((s32[]{:T(128)}, f32[2,128,128]{2,1,0:T(8,128)S(1)}, ...), condition=%wide.region_22.23_spmd.clone.clone, body=%wide.region_11.22_spmd.clone.clone.sunk | while | flops 95114432 | bytes 4842541 | solution.py:72
  239.7 9.8 %custom-call.51 = f32[2,1,64,64]{2,3,1,0:T(8,128)S(1)} custom-call(f32[2,1,64,64]{3,2,1,0:T(8,128)S(1)} %add_bitcast_fusion.5), custom_call_target="InvertDiagBlocksLowerTriangular" | custom-call | tf_op jit(solution)/shard_map/transpose(jvp(vmap()))/while/body/eval_jaxpr/jit(_solve_triangular)/triangular_solve | solution.py:43
  264.0 9.8 %custom-call.51 = f32[2,1,64,64]{2,3,1,0:T(8,128)S(1)} custom-call(f32[2,1,64,64]{3,2,1,0:T(8,128)S(1)} %add_bitcast_fusion.5), custom_call_target="InvertDiagBlocksLowerTriangular" | custom-call | tf_op jit(solution)/shard_map/transpose(jvp(vmap()))/while/body/eval_jaxpr/jit(_solve_triangular)/triangular_solve | solution.py:43
  288.3 9.8 %custom-call.51 = f32[2,1,64,64]{2,3,1,0:T(8,128)S(1)} custom-call(f32[2,1,64,64]{3,2,1,0:T(8,128)S(1)} %add_bitcast_fusion.5), custom_call_target="InvertDiagBlocksLowerTriangular" | custom-call | tf_op jit(solution)/shard_map/transpose(jvp(vmap()))/while/body/eval_jaxpr/jit(_solve_triangular)/triangular_solve | solution.py:43
  298.9 1.2 fusion.377
  312.6 9.8 %custom-call.51 = f32[2,1,64,64]{2,3,1,0:T(8,128)S(1)} custom-call(f32[2,1,64,64]{3,2,1,0:T(8,128)S(1)} %add_bitcast_fusion.5), custom_call_target="InvertDiagBlocksLowerTriangular" | custom-call | tf_op jit(solution)/shard_map/transpose(jvp(vmap()))/while/body/eval_jaxpr/jit(_solve_triangular)/triangular_solve | solution.py:43
  334.4 5.5 %convolution_convert_fusion = bf16[256,8192]{1,0:T(8,128)(2,1)} fusion(bf16[256,256]{0,1:T(8,128)(2,1)S(1)} %bitcast.660, bf16[8192,256]{1,0:T(8,128)(2,1)} %bitcast.23), kind=kOutput, calls=%fused_computation.283 | convolution fusion | flops 1075838976 | bytes 8519680 | tf_op jit(solution)/shard_map/dot_general | solution.py:153
  341.4 10.3 %all-to-all-start.1 = ((f32[32,2,2]{2,1,0:T(2,128)}), f32[32,2,2]{2,1,0:T(2,128)S(1)}, u32[]{:S(2)}, u32[]{:S(2)}) async-start(f32[32,2,2]{2,1,0:T(2,128)} %broadcast_in_dim.279), calls=%async_computation.2 | async-start | bytes 65536 | tf_op jit(solution)/shard_map/all_to_all | solution.py:18
  354.8 5.3 %all-to-all-done.1 = f32[32,2,2]{2,1,0:T(2,128)S(1)} async-done(((f32[32,2,2]{2,1,0:T(2,128)}), f32[32,2,2]{2,1,0:T(2,128)S(1)}, u32[]{:S(2)}, u32[]{:S(2)}) %all-to-all-start.1) | async-done | bytes 544 | tf_op jit(solution)/shard_map/all_to_all | solution.py:18
  360.7 83.1 %reduce-scatter.2.cloned.1.call-done = bf16[16,8192]{1,0:T(8,128)(2,1)} async-done(((bf16[256,8192]{1,0:T(8,128)(2,1)}), bf16[16,8192]{1,0:T(8,128)(2,1)}) %reduce-scatter.2.cloned.1.call-update) | async-done | bytes 262160 | tf_op jit(solution)/shard_map/reduce_scatter | solution.py:152
  (424 shorter events, 110.1 us)
Async XLA Ops:
  10.5 13.0 %copy-start.15 = (f32[2,1,2,256]{3,2,1,0:T(2,128)S(1)}, f32[2,1,2,256]{3,2,1,0:T(2,128)}, u32[]{:S(2)}) copy-start(f32[2,1,2,256]{3,2,1,0:T(2,128)} %param.23) | copy-start | bytes 12292
  10.5 13.2 %copy-start.3 = (bf16[1,256,256]{2,1,0:T(8,128)(2,1)S(1)}, bf16[1,256,256]{2,1,0:T(8,128)(2,1)}, u32[]{:S(2)}) copy-start(bf16[1,256,256]{2,1,0:T(8,128)(2,1)} %param.21) | copy-start | bytes 393220
  10.5 13.6 %copy-start.4 = (bf16[1,256,256]{2,1,0:T(8,128)(2,1)S(1)}, bf16[1,256,256]{2,1,0:T(8,128)(2,1)}, u32[]{:S(2)}) copy-start(bf16[1,256,256]{2,1,0:T(8,128)(2,1)} %param.20) | copy-start | bytes 393220
  10.5 117.8 %all-to-all-start = ((bf16[32,256,256]{2,1,0:T(8,128)(2,1)}), bf16[32,256,256]{2,1,0:T(8,128)(2,1)}, u32[]{:S(2)}, u32[]{:S(2)}) async-start(bf16[32,256,256]{2,1,0:T(8,128)(2,1)} %stack.4), calls=%async_computation | async-start | bytes 8388608 | tf_op jit(solution)/shard_map/all_to_all | solution.py:99
  22.5 3.2 copy-start.21
  22.5 105.8 %all-gather.2.cloned.1.call-start = ((), (), s32[]{:S(2)}) async-start(), calls=%async_computation.3 | async-start | bytes 4456448 | tf_op jit(solution)/shard_map/all_gather | solution.py:94
  23.2 420.6 %reduce-scatter.2.cloned.1.call-start = ((), (), s32[]{:S(2)}) async-start(), calls=%async_computation.4 | async-start | bytes 4456448 | tf_op jit(solution)/shard_map/reduce_scatter | solution.py:152
  23.5 0.7 copy-start.11
  23.9 1.8 copy-start.7
  23.9 1.7 copy-start.5
  24.2 1.4 copy-start.9
  25.7 107.9 %copy-start.17 = (f32[2]{0:T(128)}, f32[2]{0:T(128)S(1)}, u32[]{:S(2)}) copy-start(f32[2]{0:T(128)S(1)} %get-tuple-element.2979) | copy-start | bytes 28
  25.7 107.9 %copy-start.19 = (f32[2]{0:T(128)}, f32[2]{0:T(128)S(1)}, u32[]{:S(2)}) copy-start(f32[2]{0:T(128)S(1)} %get-tuple-element.2980) | copy-start | bytes 28
  128.3 7.0 %copy-start = (f32[1,1,2,128,128]{4,3,2,1,0:T(8,128)S(1)}, f32[1,1,2,128,128]{4,3,2,1,0:T(8,128)}, u32[]{:S(2)}) copy-start(f32[1,1,2,128,128]{4,3,2,1,0:T(8,128)} %param.25) | copy-start | bytes 393220
  210.1 3.1 collective-permute-start
  218.4 5.1 %collective-permute-start.1 = (bf16[2,128,128]{2,1,0:T(8,128)(2,1)S(1)}, bf16[2,128,128]{2,1,0:T(8,128)(2,1)S(1)}, u32[]{:S(2)}, u32[]{:S(2)}) collective-permute-start(bf16[2,128,128]{2,1,0:T(8,128)(2,1)S(1)} %convert_element_type.127), channel_id=1, source_target_pairs={{16,0},{32,16},{48,32},{17,1},{33,17},{49,33},{18,2},{34,18},{50,3... | collective-permute-start | bytes 196616 | tf_op jit(solution)/shard_map/ppermute | solution.py:13
  228.6 5.6 %collective-permute-start.2 = (bf16[2,128,128]{2,1,0:T(8,128)(2,1)S(1)}, bf16[2,128,128]{2,1,0:T(8,128)(2,1)S(1)}, u32[]{:S(2)}, u32[]{:S(2)}) collective-permute-start(bf16[2,128,128]{2,1,0:T(8,128)(2,1)S(1)} %convert_element_type.129), channel_id=1, source_target_pairs={{16,0},{32,16},{48,32},{17,1},{33,17},{49,33},{18,2},{34,18},{50,3... | collective-permute-start | bytes 196616 | tf_op jit(solution)/shard_map/ppermute | solution.py:13
  339.9 0.7 copy-start.13
  339.9 0.7 copy-start.18
  339.9 0.7 copy-start.20
  339.9 0.9 copy-start.22
  339.9 11.9 %copy-start.14 = (f32[4,2,64]{2,1,0:T(2,128)S(1)}, f32[4,2,64]{2,1,0:T(2,128)}, u32[]{:S(2)}) copy-start(f32[4,2,64]{2,1,0:T(2,128)} %get-tuple-element.1874) | copy-start | bytes 6148
  339.9 12.1 %copy-start.2 = (f32[4,2,64,128]{3,2,0,1:T(8,128)S(1)}, f32[4,2,64,128]{3,2,0,1:T(8,128)}, u32[]{:S(2)}) copy-start(f32[4,2,64,128]{3,2,0,1:T(8,128)} %get-tuple-element.1872) | copy-start | bytes 786436
  339.9 12.2 %copy-start.1 = (f32[4,2,64,128]{3,2,0,1:T(8,128)S(1)}, f32[4,2,64,128]{3,2,0,1:T(8,128)}, u32[]{:S(2)}) copy-start(f32[4,2,64,128]{3,2,0,1:T(8,128)} %get-tuple-element.1871) | copy-start | bytes 786436
  339.9 12.4 %copy-start.12 = (f32[1,1,2,256]{3,2,1,0:T(2,128)S(1)}, f32[1,1,2,256]{3,2,1,0:T(2,128)}, u32[]{:S(2)}) copy-start(f32[1,1,2,256]{3,2,1,0:T(2,128)} %copy-done.11) | copy-start | bytes 6148
  339.9 12.5 %copy-start.8 = (f32[2,256]{1,0:T(2,128)S(1)}, f32[2,256]{1,0:T(2,128)}, u32[]{:S(2)}) copy-start(f32[2,256]{1,0:T(2,128)} %copy-done.7) | copy-start | bytes 6148
  339.9 12.5 %copy-start.16 = (f32[2,1,2,256]{3,2,1,0:T(2,128)S(1)}, f32[2,1,2,256]{3,2,1,0:T(2,128)}, u32[]{:S(2)}) copy-start(f32[2,1,2,256]{3,2,1,0:T(2,128)} %param.23) | copy-start | bytes 12292
  339.9 12.6 %copy-start.10 = (f32[2,256]{1,0:T(2,128)S(1)}, f32[2,256]{1,0:T(2,128)}, u32[]{:S(2)}) copy-start(f32[2,256]{1,0:T(2,128)} %copy-done.9) | copy-start | bytes 6148
  340.0 12.6 %copy-start.6 = (f32[2,256]{1,0:T(2,128)S(1)}, f32[2,256]{1,0:T(2,128)}, u32[]{:S(2)}) copy-start(f32[2,256]{1,0:T(2,128)} %copy-done.5) | copy-start | bytes 6148
  341.4 18.6 %all-to-all-start.1 = ((f32[32,2,2]{2,1,0:T(2,128)}), f32[32,2,2]{2,1,0:T(2,128)S(1)}, u32[]{:S(2)}, u32[]{:S(2)}) async-start(f32[32,2,2]{2,1,0:T(2,128)} %broadcast_in_dim.279), calls=%async_computation.2 | async-start | bytes 65536 | tf_op jit(solution)/shard_map/all_to_all | solution.py:18
Sparse Core Ops, SparseCore 0:
  26.3 101.9 all-gather.1
  340.1 103.6 reduce-scatter.1
